TPU v7x, 32 devices: a whole 2x2x4 slice. The times are simulated.
32 devices in a mesh: owner: 4 (over x, core), rows: 8 (over z, y).
Axes of the slice: x: 2, y: 2, z: 4, core: 2. Of those that a mesh axis runs over, the one named last changes fastest.
Arguments:
- master_gate: float32 [64, 2048, 1024], P('owner', 'rows'), may hold values from -0.1875 to 0.1875
- second_gate: bfloat16 [64, 2048, 1024], P('owner', 'rows'), may hold values from -0.0625 to 0.0625
- master_up: float32 [64, 2048, 1024], P('owner', 'rows'), may hold values from -0.1875 to 0.1875
- second_up: bfloat16 [64, 2048, 1024], P('owner', 'rows'), may hold values from -0.0625 to 0.0625
- master_down: float32 [64, 1024, 2048], P('owner', None, 'rows'), may hold values from -0.25 to 0.25
- second_down: bfloat16 [64, 1024, 2048], P('owner', None, 'rows'), may hold values from -0.09375 to 0.09375
- router_weight: float32 [2048, 64], P('rows', 'owner'), may hold values from -0.125 to 0.125
- router_gain: float32 [2048], P('rows'), may hold values from 0.25 to 1.75
Outputs:
- final_gate: bfloat16 [64, 2048, 1024], P('owner', None, 'rows')
- final_up: bfloat16 [64, 2048, 1024], P('owner', None, 'rows')
- final_down: bfloat16 [64, 1024, 2048], P('owner', 'rows')
- scale_gate: float32 [64, 1024], P('owner', 'rows')
- scale_up: float32 [64, 1024], P('owner', 'rows')
- scale_down: float32 [64, 1024], P('owner', 'rows')
- serve_router: bfloat16 [2048, 64], replicated
All inputs are finite; a program needn't handle non-finite values.
Results may differ from a plain program's by a relative error of at most 0.001.
Values may be sent and summed in bfloat16 or wider, within the bound.
A program may use at most 192 MiB of HBM per device.

v0:
```python
import jax
import jax.numpy as jnp
from jax import lax
from jax.experimental import pallas as pl
from jax.experimental.pallas import tpu as pltpu
from jax.sharding import PartitionSpec as P


def narrow_kernel(master_ref, second_ref, scale_ref, out_ref):
    parts, _, _, width = out_ref.shape
    for part in range(parts):
        columns = slice(part * width, (part + 1) * width)
        merged = master_ref[0, :, columns] + second_ref[0, :, columns].astype(jnp.float32)
        out_ref[part, 0] = (merged / scale_ref[0, :, columns]).astype(jnp.bfloat16)


def narrow_columns(master, second, scale, parts):
    experts, depth, columns = master.shape
    width = columns // parts
    size = experts * depth * columns
    return pl.pallas_call(
        narrow_kernel,
        grid=(experts,),
        out_shape=jax.ShapeDtypeStruct((parts, experts, depth, width), jnp.bfloat16),
        in_specs=[
            pl.BlockSpec((1, depth, columns), lambda e: (e, 0, 0)),
            pl.BlockSpec((1, depth, columns), lambda e: (e, 0, 0)),
            pl.BlockSpec((1, 1, columns), lambda e: (e, 0, 0)),
        ],
        out_specs=pl.BlockSpec((parts, 1, depth, width), lambda e: (0, e, 0, 0)),
        compiler_params=pltpu.CompilerParams(vmem_limit_bytes=24 * 1024 * 1024),
        cost_estimate=pl.CostEstimate(flops=4 * size, bytes_accessed=8 * size, transcendentals=0),
    )(master, second, jnp.expand_dims(scale, 1))


def exchange_columns(narrow):
    parts, experts, depth, width = narrow.shape
    arrived = lax.all_to_all(narrow, "rows", split_axis=0, concat_axis=0, tiled=True)
    return arrived.transpose(1, 0, 2, 3).reshape(experts, parts * depth, width)


def body(
    master_gate,
    second_gate,
    master_up,
    second_up,
    master_down,
    second_down,
    router_weight,
    router_gain,
):
    parts = lax.axis_size("rows")
    merged_gate = master_gate + second_gate.astype(jnp.float32)
    merged_up = master_up + second_up.astype(jnp.float32)
    merged_down = master_down + second_down.astype(jnp.float32)
    total_gate, total_up, total_down = (
        jnp.sum(lax.all_gather(part, "rows"), axis=0)
        for part in (
            jnp.sum(merged_gate * merged_gate, axis=1),
            jnp.sum(merged_up * merged_up, axis=1),
            jnp.sum(merged_down * merged_down, axis=2),
        )
    )
    part_router = (router_weight * router_gain[:, None]).astype(jnp.bfloat16)
    row_router = lax.all_gather(part_router, "rows", axis=0, tiled=True)
    serve_router = lax.all_gather(row_router, "owner", axis=1, tiled=True)
    total_gate, total_up, total_down, serve_router = lax.optimization_barrier(
        (total_gate, total_up, total_down, serve_router)
    )
    scale_gate = jnp.sqrt(total_gate)
    scale_up = jnp.sqrt(total_up)
    scale_down = jnp.sqrt(total_down)
    final_gate = exchange_columns(narrow_columns(master_gate, second_gate, scale_gate, parts))
    final_up = exchange_columns(narrow_columns(master_up, second_up, scale_up, parts))
    narrow_down = (merged_down / jnp.expand_dims(scale_down, 2)).astype(jnp.bfloat16)
    final_down = lax.all_to_all(narrow_down, "rows", split_axis=1, concat_axis=2, tiled=True)
    scale_gate = lax.dynamic_slice_in_dim(
        scale_gate, lax.axis_index("rows") * final_gate.shape[2], final_gate.shape[2], axis=1
    )
    scale_up = lax.dynamic_slice_in_dim(
        scale_up, lax.axis_index("rows") * final_up.shape[2], final_up.shape[2], axis=1
    )
    scale_down = lax.dynamic_slice_in_dim(
        scale_down, lax.axis_index("rows") * final_down.shape[1], final_down.shape[1], axis=1
    )
    return (final_gate, final_up, final_down, scale_gate, scale_up, scale_down, serve_router)


def solution(mesh):
    placed = (
        P("owner", "rows", None),
        P("owner", "rows", None),
        P("owner", "rows", None),
        P("owner", "rows", None),
        P("owner", None, "rows"),
        P("owner", None, "rows"),
        P("rows", "owner"),
        P("rows"),
    )
    return jax.shard_map(
        body,
        mesh=mesh,
        in_specs=placed,
        out_specs=(
            P("owner", None, "rows"),
            P("owner", None, "rows"),
            P("owner", "rows", None),
            P("owner", "rows"),
            P("owner", "rows"),
            P("owner", "rows"),
            P(),
        ),
        check_vma=False,
    )
```

profile of v0, /device:TPU:0, one launch (start us, length us, event | category | flops | bytes accessed | tf_op | source)
XLA Modules:
  0.0 748.5 jit_solution(5571216798836163910)
XLA Ops:
  0.6 0.0 slice-start
  0.6 0.0 copy-start.4
  0.7 0.9 multiply_convert_fusion
  1.5 32.5 %all_gather.30 = bf16[2048,16]{0,1:T(8,128)(2,1)S(1)} all-gather(bf16[256,16]{0,1:T(8,128)(2,1)S(1)} %multiply_convert_fusion), channel_id=1, replica_groups=mesh['owner'=4,'rows'=8] {'rows'}, dimensions={0}, use_global_device_ids=true | all-gather | bytes 73728 | tf_op jit(solution)/shard_map/all_gather | solution.py:65
  34.0 5.8 all_gather.31
  39.8 0.0 slice-start.1
  39.8 9.3 %multiply_reduce_fusion.1 = f32[16,1024]{1,0:T(8,128)S(1)} fusion(f32[16,256,1024]{2,1,0:T(8,128)} %master_ref.3, bf16[16,256,1024]{2,1,0:T(8,128)(2,1)} %second_ref.3), kind=kLoop, calls=%fused_computation.3 | loop fusion | flops 16760832 | bytes 25231360 | tf_op jit(solution)/shard_map/reduce_sum | solution.py:60
  49.1 31.5 %all-gather.1 = f32[128,1024]{1,0:T(8,128)S(1)} all-gather(f32[16,1024]{1,0:T(8,128)S(1)} %multiply_reduce_fusion.1), channel_id=3, replica_groups=mesh['owner'=4,'rows'=8] {'rows'}, dimensions={0}, use_global_device_ids=true | all-gather | bytes 589824 | tf_op jit(solution)/shard_map/all_gather | solution.py:57
  80.6 0.0 slice-done
  80.6 0.0 copy-done.4
  80.6 0.0 slice-done.1
  80.7 2.8 multiply_reduce_fusion.2
  83.5 31.2 %all-gather = f32[128,1024]{1,0:T(8,128)S(1)} all-gather(f32[16,1024]{1,0:T(8,128)S(1)} %multiply_reduce_fusion.2), channel_id=2, replica_groups=mesh['owner'=4,'rows'=8] {'rows'}, dimensions={0}, use_global_device_ids=true | all-gather | bytes 589824 | tf_op jit(solution)/shard_map/all_gather | solution.py:57
  114.8 24.2 %multiply_reduce_fusion = f32[16,1024]{0,1:T(8,128)S(1)} fusion(f32[16,1024,256]{2,1,0:T(8,128)} %param.12, bf16[16,1024,256]{2,1,0:T(8,128)(2,1)} %param.13), kind=kLoop, calls=%fused_computation.2 | loop fusion | flops 16760832 | bytes 25231360 | tf_op jit(solution)/shard_map/reduce_sum | solution.py:61
  139.0 0.2 copy.47
  139.2 31.4 %all-gather.2 = f32[128,1024]{1,0:T(8,128)S(1)} all-gather(f32[16,1024]{1,0:T(8,128)S(1)} %copy.47), channel_id=4, replica_groups=mesh['owner'=4,'rows'=8] {'rows'}, dimensions={0}, use_global_device_ids=true | all-gather | bytes 589824 | tf_op jit(solution)/shard_map/all_gather | solution.py:57
  170.6 0.2 copy.50
  170.8 23.8 %divide_convert_fusion = bf16[16,1024,256]{2,0,1:T(8,128)(2,1)} fusion(f32[16,1024,256]{2,1,0:T(8,128)} %param.12, f32[16,1024]{0,1:T(8,128)S(1)} %copy.50, bf16[16,1024,256]{2,1,0:T(8,128)(2,1)} %param.13), kind=kLoop, calls=%fused_computation.1 | loop fusion | flops 16777216 | bytes 33619968 | tf_op jit(solution)/shard_map/convert_element_type | solution.py:75
  194.6 5.8 all-to-all-start.2
  200.5 0.0 copy-start
  200.5 3.4 copy-done
  203.9 12.1 %shard_map.136 = bf16[8,16,256,128]{3,2,1,0:T(8,128)(2,1)S(1)} custom-call(f32[16,256,1024]{2,1,0:T(8,128)} %master_ref.3, bf16[16,256,1024]{2,1,0:T(8,128)(2,1)S(1)} %copy-done, f32[16,1,1024]{2,1,0:T(1,128)S(1)} %broadcast_in_dim.9.scale_ref), custom_call_target="tpu_custom_call" | custom-call | flops 16777216 | bytes 33554432 | tf_op jit(solution)/shard_map/pallas_call | solution.py:21
  216.0 0.0 copy-start.3
  216.0 3.4 copy-done.3
  219.4 146.6 %all-to-all-done.2 = bf16[16,1024,256]{2,0,1:T(8,128)(2,1)} async-done(((bf16[16,1024,256]{2,0,1:T(8,128)(2,1)}), bf16[16,1024,256]{2,0,1:T(8,128)(2,1)}, u32[]{:S(2)}, u32[]{:S(2)}) %all-to-all-start.2) | async-done | bytes 8388640 | tf_op jit(solution)/shard_map/all_to_all | solution.py:76
  366.1 5.0 all-to-all-start.1
  371.2 0.0 copy-start.1
  371.2 3.4 copy-done.1
  374.6 12.1 %shard_map.135 = bf16[8,16,256,128]{3,2,1,0:T(8,128)(2,1)S(1)} custom-call(f32[16,256,1024]{2,1,0:T(8,128)} %master_ref.2, bf16[16,256,1024]{2,1,0:T(8,128)(2,1)S(1)} %copy-done.1, f32[16,1,1024]{2,1,0:T(1,128)S(1)} %broadcast_in_dim.8.scale_ref), custom_call_target="tpu_custom_call" | custom-call | flops 16777216 | bytes 33554432 | tf_op jit(solution)/shard_map/pallas_call | solution.py:21
  386.7 0.0 copy-start.2
  386.7 3.4 copy-done.2
  390.1 162.7 %all-to-all-done.1 = bf16[8,16,256,128]{3,2,1,0:T(8,128)(2,1)} async-done(((bf16[8,16,256,128]{3,2,1,0:T(8,128)(2,1)}), bf16[8,16,256,128]{3,2,1,0:T(8,128)(2,1)}, u32[]{:S(2)}, u32[]{:S(2)}) %all-to-all-start.1) | async-done | bytes 8388640 | tf_op jit(solution)/shard_map/all_to_all | solution.py:38
  552.8 5.2 all-to-all-start
  558.0 0.6 constant_dynamic-slice_fusion.2
  558.6 0.6 constant_dynamic-slice_fusion
  559.2 11.5 %copy.51 = bf16[16,128,8,256]{3,2,1,0:T(8,128)(2,1)} copy(bf16[16,128,8,256]{3,0,1,2:T(8,128)(2,1)} %bitcast.8) | data formatting | bytes 16777216 | tf_op jit(solution)/shard_map/all_to_all | solution.py:76
  570.8 13.4 %all_to_all.24 = bf16[16,128,2048]{2,1,0:T(8,128)(2,1)} reshape(bf16[16,128,8,256]{3,2,1,0:T(8,128)(2,1)} %copy.51) | data formatting | bytes 16777216 | tf_op jit(solution)/shard_map/all_to_all | solution.py:76
  584.2 7.9 %copy.49 = bf16[16,8,256,128]{3,2,1,0:T(8,128)(2,1)} copy(bf16[16,8,256,128]{3,2,0,1:T(8,128)(2,1)} %bitcast.5) | data formatting | bytes 16777216 | tf_op jit(solution)/shard_map/transpose | solution.py:39
  592.1 147.8 %all-to-all-done = bf16[8,16,256,128]{3,2,1,0:T(8,128)(2,1)} async-done(((bf16[8,16,256,128]{3,2,1,0:T(8,128)(2,1)}), bf16[8,16,256,128]{3,2,1,0:T(8,128)(2,1)}, u32[]{:S(2)}, u32[]{:S(2)}) %all-to-all-start) | async-done | bytes 8388640 | tf_op jit(solution)/shard_map/all_to_all | solution.py:38
  739.9 7.9 %copy.48 = bf16[16,8,256,128]{3,2,1,0:T(8,128)(2,1)} copy(bf16[16,8,256,128]{3,2,0,1:T(8,128)(2,1)} %bitcast.3) | data formatting | bytes 16777216 | tf_op jit(solution)/shard_map/transpose | solution.py:39
  747.8 0.7 copy.60
  (9 shorter events, 0.2 us)
Async XLA Ops:
  0.6 80.0 %slice-start = ((s8[8388608]{0:T(1024)(128)(4,1)}), s8[4194304]{0:T(1024)(128)(4,1)S(1)}, s32[]{:S(2)}) async-start(s8[8388608]{0:T(1024)(128)(4,1)} %bitcast.12), calls=%async_computation.3 | async-start | bytes 8388608
  0.6 80.0 %copy-start.4 = (f32[16,256,1024]{2,1,0:T(8,128)S(1)}, f32[16,256,1024]{2,1,0:T(8,128)}, u32[]{:S(2)}) copy-start(f32[16,256,1024]{2,1,0:T(8,128)} %master_ref.2) | copy-start | bytes 50331652
  39.8 40.9 %slice-start.1 = ((s8[8388608]{0:T(1024)(128)(4,1)}), s8[4194304]{0:T(1024)(128)(4,1)S(1)}, s32[]{:S(2)}) async-start(s8[8388608]{0:T(1024)(128)(4,1)} %bitcast.12), calls=%async_computation.4 | async-start | bytes 8388608
  194.6 171.4 %all-to-all-start.2 = ((bf16[16,1024,256]{2,0,1:T(8,128)(2,1)}), bf16[16,1024,256]{2,0,1:T(8,128)(2,1)}, u32[]{:S(2)}, u32[]{:S(2)}) async-start(bf16[16,1024,256]{2,0,1:T(8,128)(2,1)} %divide_convert_fusion), calls=%async_computation.2 | async-start | bytes 16777216 | tf_op jit(solution)/shard_map/all_to_all | solution.py:76
  200.5 3.4 copy-start
  216.0 3.4 copy-start.3
  366.1 186.8 %all-to-all-start.1 = ((bf16[8,16,256,128]{3,2,1,0:T(8,128)(2,1)}), bf16[8,16,256,128]{3,2,1,0:T(8,128)(2,1)}, u32[]{:S(2)}, u32[]{:S(2)}) async-start(bf16[8,16,256,128]{3,2,1,0:T(8,128)(2,1)} %copy-done.3), calls=%async_computation.1 | async-start | bytes 16777216 | tf_op jit(solution)/shard_map/all_to_all | solution.py:38
  371.2 3.4 copy-start.1
  386.7 3.4 copy-start.2
  552.8 187.1 %all-to-all-start = ((bf16[8,16,256,128]{3,2,1,0:T(8,128)(2,1)}), bf16[8,16,256,128]{3,2,1,0:T(8,128)(2,1)}, u32[]{:S(2)}, u32[]{:S(2)}) async-start(bf16[8,16,256,128]{3,2,1,0:T(8,128)(2,1)} %copy-done.2), calls=%async_computation | async-start | bytes 16777216 | tf_op jit(solution)/shard_map/all_to_all | solution.py:38
where the time goes:
time: 750 us; the launch traced here: 749 us
  waiting for transfers between devices  457 us (61%)
  blocking collectives  132 us (18%)
  other arithmetic  61.2 us (8%)
  local copies, waits for them, and re-layouts  56.7 us (8%)
  Pallas kernels  24.2 us (3%)
  starting transfers between devices  16.1 us (2%)
    all_to_all x2, waiting for transfers between devices, exchange_columns(): lax.all_to_all(narrow, 'rows', split_axis=0, concat_axis=0, tiled=True)  311 us
    all_to_all x1, waiting for transfers between devices, body(): lax.all_to_all(narrow_down, 'rows', split_axis=1, concat_axis=2, tiled=True)  147 us
    all_gather x3, blocking collectives, body(): lax.all_gather(part, 'rows')  94.1 us
    all_gather x1, blocking collectives, body(): row_router = lax.all_gather(part_router, 'rows', axis=0, tiled=True)  32.5 us
    all_to_all x2, local copies, waits for them, and re-layouts, body(): lax.all_to_all(narrow_down, 'rows', split_axis=1, concat_axis=2, tiled=True)  25 us
    reduce_sum x1, other arithmetic, body(): jnp.sum(merged_down * merged_down, axis=2)  24.2 us
    pallas_call x2, Pallas kernels, narrow_columns(): pl.pallas_call(narrow_kernel, grid=(experts,), out_shape=jax.ShapeDtypeSt...  24.2 us
    convert_element_type x1, other arithmetic, body(): (merged_down / jnp.expand_dims(scale_down, 2)).astype(jnp.bfloat16)  23.8 us
  transfers between devices with their start and end apart: 3, of which 3 were waited for; matrix products, arithmetic and copies ran while one was open for 3% of the time, Pallas kernels for 3%

commit v1 on v0

--- a/solution.py
+++ b/solution.py
@@ -39,6 +39,480 @@
     return arrived.transpose(1, 0, 2, 3).reshape(experts, parts * depth, width)
 
 
+MESH = pl.DeviceIdType.MESH
+LANES = 128
+SLOTS = 3
+FIRST = 6
+EARLY = 3
+
+
+def serve_kernel(
+    master_gate,
+    second_gate,
+    master_up,
+    second_up,
+    master_down,
+    second_down,
+    router_weight,
+    router_gain,
+    final_wide,
+    final_down,
+    scale_gate,
+    scale_up,
+    scale_down,
+    serve_router,
+    wide_master,
+    wide_second,
+    tall_master,
+    tall_second,
+    wide_send,
+    tall_send,
+    first_sums,
+    first_scales,
+    sums,
+    half_sums,
+    half_total,
+    other_total,
+    scales,
+    weight_vmem,
+    gain_vmem,
+    wide_sem,
+    tall_sem,
+    router_sem,
+    bulk_sent,
+    bulk_arrived,
+    first_sent,
+    first_arrived,
+    near_sent,
+    near_arrived,
+    across_sent,
+    across_arrived,
+    back_sent,
+    back_arrived,
+    route_sent,
+    route_arrived,
+    owner_sent,
+    owner_arrived,
+):
+    rows = lax.axis_size("rows")
+    owners = lax.axis_size("owner")
+    half = rows // 2
+    per_rank = rows // half
+    me = lax.axis_index("rows")
+    owner = lax.axis_index("owner")
+    rank = lax.rem(me, half)
+    base = me - rank
+    mirror = lax.rem(me + half, rows)
+    experts, depth, _ = master_gate.shape
+    width = final_wide.shape[2]
+    tall = final_down.shape[1]
+    across = master_down.shape[2]
+
+    def row_peer(step):
+        return lax.rem(me + step, rows)
+
+    def half_peer(step):
+        return base + lax.rem(rank + step, half)
+
+    def owner_peer(step):
+        return lax.rem(owner + step, owners)
+
+    barrier = pltpu.get_barrier_semaphore()
+    for step in range(1, rows):
+        pl.semaphore_signal(barrier, inc=1, device_id={"rows": row_peer(step)}, device_id_type=MESH)
+    for step in range(1, owners):
+        pl.semaphore_signal(barrier, inc=1, device_id={"owner": owner_peer(step)}, device_id_type=MESH)
+
+    def remote(source, target, sent, arrived, place):
+        return pltpu.make_async_remote_copy(
+            src_ref=source,
+            dst_ref=target,
+            send_sem=sent,
+            recv_sem=arrived,
+            device_id=place,
+            device_id_type=MESH,
+        )
+
+    def fetch(pair, buffers, sems, expert, slot):
+        return [
+            pltpu.make_async_copy(pair[i].at[expert], buffers[i].at[slot], sems.at[i, slot])
+            for i in range(2)
+        ]
+
+    def ahead(pair, buffers, sems, first, count):
+        for i in range(min(SLOTS, count)):
+            for copy in fetch(pair, buffers, sems, first + i, i):
+                copy.start()
+
+    def run(pair, buffers, sems, first, count, work):
+        def step(i, _):
+            slot = lax.rem(i, SLOTS)
+            for copy in fetch(pair, buffers, sems, first + i, slot):
+                copy.wait()
+            work(first + i, slot)
+
+            @pl.when(i + SLOTS < count)
+            def _():
+                for copy in fetch(pair, buffers, sems, first + i + SLOTS, slot):
+                    copy.start()
+
+            return 0
+
+        lax.fori_loop(0, count, step, 0)
+
+    wide = (wide_master, wide_second)
+    high = (tall_master, tall_second)
+    gate = (master_gate, second_gate)
+    up = (master_up, second_up)
+    down = (master_down, second_down)
+
+    def wide_block(slot, part):
+        columns = pl.ds(pl.multiple_of(part * width, width), width)
+        return wide_master[slot, :, columns] + wide_second[slot, :, columns].astype(jnp.float32)
+
+    def tall_block(slot, part):
+        lines = pl.ds(pl.multiple_of(part * tall, tall), tall)
+        return tall_master[slot, lines, :] + tall_second[slot, lines, :].astype(jnp.float32)
+
+    def wide_total(slot, part):
+        merged = wide_block(slot, part)
+        return jnp.sum(merged * merged, axis=0, keepdims=True)
+
+    def tall_total(slot, part):
+        merged = tall_block(slot, part)
+        square = merged * merged
+        narrow = square[:, :LANES]
+        for at in range(LANES, across, LANES):
+            narrow = narrow + square[:, at : at + LANES]
+        return jnp.sum(narrow.T, axis=0, keepdims=True)
+
+    def sum_first(expert, slot):
+        for part in range(rows):
+            first_sums[me, expert, part : part + 1, :] = wide_total(slot, part)
+
+    def sum_rest(total_of, offset):
+        def work(expert, slot):
+            for part in range(rows):
+                sums[part, pl.ds(offset + expert, 1), :] = total_of(slot, part)
+
+        return work
+
+    def first_scale(expert, part):
+        return first_scales[expert, pl.ds(part, 1), :]
+
+    def rest_scale(offset):
+        return lambda expert, part: scales[part, pl.ds(offset + expert, 1), :]
+
+    my_lines = pl.ds(pl.multiple_of(me * depth, depth), depth)
+    my_columns = pl.ds(pl.multiple_of(me * across, across), across)
+
+    def narrow_wide(scale_of, which):
+        def work(expert, slot):
+            at = which * experts + expert
+
+            def block(i, _):
+                step = rows - 1 - i
+                part = row_peer(step)
+                value = wide_block(slot, part) / scale_of(expert, part)
+                wide_send[at, step - 1] = value.astype(jnp.bfloat16)
+                remote(
+                    wide_send.at[at, step - 1],
+                    final_wide.at[at, my_lines, :],
+                    bulk_sent.at[which],
+                    bulk_arrived.at[which],
+                    {"rows": part},
+                ).start()
+                return 0
+
+            lax.fori_loop(0, rows - 1, block, 0)
+            own = wide_block(slot, me) / scale_of(expert, me)
+            final_wide[at, my_lines, :] = own.astype(jnp.bfloat16)
+
+        return work
+
+    def narrow_tall(slot, part, line):
+        merged = tall_block(slot, part)
+        scale = jnp.broadcast_to(line, (tall, LANES)).T
+        scale = jnp.concatenate([scale] * (across // LANES), axis=1)
+        return (merged / scale).astype(jnp.bfloat16)
+
+    def narrow_down(expert, slot):
+        scale_of = rest_scale(2 * experts)
+
+        def block(i, _):
+            step = rows - 1 - i
+            part = row_peer(step)
+            tall_send[expert, step - 1] = narrow_tall(slot, part, scale_of(expert, part))
+            remote(
+                tall_send.at[expert, step - 1],
+                final_down.at[expert, :, my_columns],
+                bulk_sent.at[2],
+                bulk_arrived.at[2],
+                {"rows": part},
+            ).start()
+            return 0
+
+        lax.fori_loop(0, rows - 1, block, 0)
+        final_down[expert, :, my_columns] = narrow_tall(slot, me, scale_of(expert, me))
+
+    ahead(gate, wide, wide_sem, 0, FIRST)
+    fetch_router = [
+        pltpu.make_async_copy(router_weight, weight_vmem, router_sem.at[0]),
+        pltpu.make_async_copy(router_gain, gain_vmem, router_sem.at[1]),
+    ]
+    for copy in fetch_router:
+        copy.start()
+    sums[...] = jnp.zeros_like(sums)
+    run(gate, wide, wide_sem, 0, FIRST, sum_first)
+    ahead(gate, wide, wide_sem, 0, EARLY)
+    pl.semaphore_wait(barrier, rows - 1 + owners - 1)
+    first_copies = [
+        remote(
+            first_sums.at[me],
+            first_sums.at[me],
+            first_sent.at[step - 1],
+            first_arrived.at[step - 1],
+            {"rows": row_peer(step)},
+        )
+        for step in range(1, rows)
+    ]
+    for copy in first_copies:
+        copy.start()
+
+    for copy in fetch_router:
+        copy.wait()
+    mine = weight_vmem.shape[0]
+    my_experts = pl.ds(pl.multiple_of(owner * mine, mine), mine)
+    here = pl.ds(pl.multiple_of(me * depth, depth), depth)
+    there = pl.ds(pl.multiple_of(mirror * depth, depth), depth)
+    serve_router[my_experts, here] = (weight_vmem[...] * gain_vmem[...]).astype(jnp.bfloat16)
+    my_route = serve_router.at[my_experts, here]
+    other_route = serve_router.at[my_experts, there]
+    route_copies = [remote(my_route, my_route, route_sent.at[0], route_arrived.at[0], {"rows": mirror})]
+    route_copies[0].start()
+
+    for copy in first_copies:
+        copy.wait_recv()
+    total = first_sums[0]
+    for part in range(1, rows):
+        total = total + first_sums[part]
+    first_scales[...] = jnp.sqrt(total)
+    narrow_first = narrow_wide(first_scale, 0)
+    run(gate, wide, wide_sem, 0, EARLY, narrow_first)
+
+    sum_gate = sum_rest(wide_total, 0)
+    sum_up = sum_rest(wide_total, experts)
+    sum_down = sum_rest(tall_total, 2 * experts)
+    ahead(gate, wide, wide_sem, FIRST, experts - FIRST)
+    ahead(down, high, tall_sem, 0, experts)
+    run(gate, wide, wide_sem, FIRST, experts - FIRST, sum_gate)
+    ahead(up, wide, wide_sem, 0, experts)
+    run(down, high, tall_sem, 0, experts, sum_down)
+    run(up, wide, wide_sem, 0, experts, sum_up)
+
+    ahead(gate, wide, wide_sem, EARLY, 1)
+    near_copies = []
+    for step in range(1, half):
+        peer = half_peer(step)
+        peer_rank = lax.rem(rank + step, half)
+        near_copies.append(
+            remote(
+                sums.at[pl.ds(peer_rank * per_rank, per_rank)],
+                half_sums.at[rank],
+                near_sent.at[step - 1],
+                near_arrived.at[step - 1],
+                {"rows": peer},
+            )
+        )
+        near_copies[-1].start()
+    half_sums[rank] = sums[pl.ds(rank * per_rank, per_rank)]
+    run(gate, wide, wide_sem, EARLY, 1, narrow_first)
+    ahead(gate, wide, wide_sem, EARLY + 1, 1)
+    for copy in near_copies:
+        copy.wait_recv()
+    total = half_sums[0]
+    for part in range(1, half):
+        total = total + half_sums[part]
+    half_total[...] = total
+    across_copy = remote(half_total, other_total, across_sent.at[0], across_arrived.at[0], {"rows": mirror})
+    across_copy.start()
+    route_copies[0].wait_recv()
+    for step in range(1, half):
+        for i, route in enumerate((my_route, other_route)):
+            at = 1 + 2 * (step - 1) + i
+            route_copies.append(
+                remote(route, route, route_sent.at[at], route_arrived.at[at], {"rows": half_peer(step)})
+            )
+            route_copies[-1].start()
+    run(gate, wide, wide_sem, EARLY + 1, 1, narrow_first)
+    ahead(gate, wide, wide_sem, EARLY + 2, FIRST - EARLY - 2)
+    across_copy.wait_recv()
+    my_parts = pl.ds(rank * per_rank, per_rank)
+    scales[my_parts] = jnp.sqrt(half_total[...] + other_total[...])
+    back_copies = [
+        remote(
+            scales.at[my_parts],
+            scales.at[my_parts],
+            back_sent.at[step - 1],
+            back_arrived.at[step - 1],
+            {"rows": half_peer(step)},
+        )
+        for step in range(1, half)
+    ]
+    for copy in back_copies:
+        copy.start()
+    run(gate, wide, wide_sem, EARLY + 2, FIRST - EARLY - 2, narrow_first)
+    ahead(gate, wide, wide_sem, FIRST, experts - FIRST)
+    ahead(down, high, tall_sem, 0, experts)
+    for copy in route_copies[1:]:
+        copy.wait_recv()
+    owner_route = serve_router.at[my_experts, :]
+    owner_copies = [
+        remote(
+            owner_route,
+            owner_route,
+            owner_sent.at[step - 1],
+            owner_arrived.at[step - 1],
+            {"owner": owner_peer(step)},
+        )
+        for step in range(1, owners)
+    ]
+    for copy in owner_copies:
+        copy.start()
+    for copy in back_copies:
+        copy.wait_recv()
+
+    run(gate, wide, wide_sem, FIRST, experts - FIRST, narrow_wide(rest_scale(0), 0))
+    ahead(up, wide, wide_sem, 0, experts)
+    run(up, wide, wide_sem, 0, experts, narrow_wide(rest_scale(experts), 1))
+    run(down, high, tall_sem, 0, experts, narrow_down)
+
+    scale_gate[...] = scales[me, 0:experts]
+    for expert in range(FIRST):
+        scale_gate[expert : expert + 1, :] = first_scale(expert, me)
+    scale_up[...] = scales[me, experts : 2 * experts]
+    scale_down[...] = scales[me, 2 * experts : 3 * experts]
+
+    for copy in owner_copies:
+        copy.wait_recv()
+    for copies in (first_copies, route_copies, near_copies, [across_copy], back_copies, owner_copies):
+        for copy in copies:
+            copy.wait_send()
+    incoming = pl.ds(0, (rows - 1) * depth)
+    arrived = (
+        final_wide.at[pl.ds(0, experts), incoming, :],
+        final_wide.at[pl.ds(experts, experts), incoming, :],
+        final_down.at[:, :, pl.ds(0, (rows - 1) * across)],
+    )
+    sent = (wide_send.at[pl.ds(0, experts)], wide_send.at[pl.ds(experts, experts)], tall_send)
+    place = {"rows": row_peer(1)}
+    for which in range(3):
+        remote(sent[which], sent[which], bulk_sent.at[which], bulk_arrived.at[which], place).wait_send()
+    for which in range(3):
+        remote(arrived[which], arrived[which], bulk_sent.at[which], bulk_arrived.at[which], place).wait_recv()
+
+
+def serve(
+    master_gate,
+    second_gate,
+    master_up,
+    second_up,
+    master_down,
+    second_down,
+    router_weight,
+    router_gain,
+):
+    rows = lax.axis_size("rows")
+    owners = lax.axis_size("owner")
+    half = rows // 2
+    per_rank = rows // half
+    experts, depth, columns = master_gate.shape
+    _, lines, across = master_down.shape
+    width = columns // rows
+    tall = lines // rows
+    mine = router_weight.shape[1]
+    f32, bf16, dma = jnp.float32, jnp.bfloat16, pltpu.SemaphoreType.DMA
+    chunks = 3 * experts
+    hbm = pl.BlockSpec(memory_space=pltpu.HBM)
+    vmem = pl.BlockSpec(memory_space=pltpu.VMEM)
+    size = 3 * experts * depth * columns
+    outs = pl.pallas_call(
+        serve_kernel,
+        out_shape=(
+            pltpu.VMEM((2 * experts, rows * depth, width), bf16),
+            pltpu.VMEM((experts, tall, rows * across), bf16),
+            jax.ShapeDtypeStruct((experts, width), f32),
+            jax.ShapeDtypeStruct((experts, width), f32),
+            jax.ShapeDtypeStruct((experts, tall), f32),
+            jax.ShapeDtypeStruct((owners * mine, rows * depth), bf16),
+        ),
+        in_specs=[hbm] * 8,
+        out_specs=(vmem,) * 6,
+        scratch_shapes=[
+            pltpu.VMEM((SLOTS, depth, columns), f32),
+            pltpu.VMEM((SLOTS, depth, columns), bf16),
+            pltpu.VMEM((SLOTS, lines, across), f32),
+            pltpu.VMEM((SLOTS, lines, across), bf16),
+            pltpu.VMEM((2 * experts, rows - 1, depth, width), bf16),
+            pltpu.VMEM((experts, rows - 1, tall, across), bf16),
+            pltpu.VMEM((rows, FIRST, rows, LANES), f32),
+            pltpu.VMEM((FIRST, rows, LANES), f32),
+            pltpu.VMEM((rows, chunks, LANES), f32),
+            pltpu.VMEM((half, per_rank, chunks, LANES), f32),
+            pltpu.VMEM((per_rank, chunks, LANES), f32),
+            pltpu.VMEM((per_rank, chunks, LANES), f32),
+            pltpu.VMEM((rows, chunks, LANES), f32),
+            pltpu.VMEM((mine, depth), f32),
+            pltpu.VMEM((1, depth), f32),
+            dma((2, SLOTS)),
+            dma((2, SLOTS)),
+            dma((2,)),
+            dma((3,)),
+            dma((3,)),
+            dma((rows - 1,)),
+            dma((rows - 1,)),
+            dma((half - 1,)),
+            dma((half - 1,)),
+            dma((1,)),
+            dma((1,)),
+            dma((half - 1,)),
+            dma((half - 1,)),
+            dma((2 * half - 1,)),
+            dma((2 * half - 1,)),
+            dma((owners - 1,)),
+            dma((owners - 1,)),
+        ],
+        compiler_params=pltpu.CompilerParams(
+            collective_id=0, has_side_effects=True, vmem_limit_bytes=34 * 1024 * 1024
+        ),
+        cost_estimate=pl.CostEstimate(flops=8 * size, bytes_accessed=12 * size, transcendentals=0),
+    )(
+        master_gate,
+        second_gate,
+        master_up,
+        second_up,
+        master_down,
+        second_down,
+        router_weight.T,
+        jnp.expand_dims(router_gain, 0),
+    )
+    final_gate, final_up = outs[0][:experts], outs[0][experts:]
+    return (final_gate, final_up, *outs[1:5], outs[5].T)
+
+
+def serve_fits(experts, depth, columns, lines, across, mine, rows):
+    return (
+        rows == 8
+        and columns // rows == LANES
+        and lines // rows == LANES
+        and across % LANES == 0
+        and depth % LANES == 0
+        and experts % 16 == 0
+        and mine % 16 == 0
+        and experts > FIRST
+    )
+
+
 def body(
     master_gate,
     second_gate,
@@ -50,6 +524,17 @@
     router_gain,
 ):
     parts = lax.axis_size("rows")
+    if serve_fits(*master_gate.shape, *master_down.shape[1:], router_weight.shape[1], parts):
+        return serve(
+            master_gate,
+            second_gate,
+            master_up,
+            second_up,
+            master_down,
+            second_down,
+            router_weight,
+            router_gain,
+        )
     merged_gate = master_gate + second_gate.astype(jnp.float32)
     merged_up = master_up + second_up.astype(jnp.float32)
     merged_down = master_down + second_down.astype(jnp.float32)

time: 750 us -> 572 us (0.76)
  Pallas kernels: 24.2 us -> 559 us
  waiting for transfers between devices: 457 us -> 0 us
  blocking collectives: 132 us -> 0 us
  other arithmetic: 61.2 us -> 0 us
  local copies, waits for them, and re-layouts: 56.7 us -> 12.1 us
  starting transfers between devices: 16.1 us -> 0 us
    pallas_call x2 -> x1, Pallas kernels: 24.2 us -> 559 us  [serve(): pl.pallas_call(serve_kernel, out_shape=(pltpu.VMEM((2 * experts, rows * d...]
    all_to_all x3 -> x0, waiting for transfers between devices: 457 us -> none  [the longest x2 311 us: exchange_columns(): lax.all_to_all(narrow, 'rows', split_axis=0, concat_axis=0, tiled=True)]
    all_gather x5 -> x0, blocking collectives: 132 us -> none  [the longest x3 94.1 us: body(): lax.all_gather(part, 'rows')]
    reduce_sum x6 -> x0, other arithmetic: 36.5 us -> none  [the longest x1 24.2 us: body(): jnp.sum(merged_down * merged_down, axis=2)]
    all_to_all x2 -> x0, local copies, waits for them, and re-layouts: 25 us -> none  [body(): lax.all_to_all(narrow_down, 'rows', split_axis=1, concat_axis=2, tiled=True)]
    convert_element_type x2 -> x0, other arithmetic: 24.7 us -> none  [the longest x1 23.8 us: body(): (merged_down / jnp.expand_dims(scale_down, 2)).astype(jnp.bfloat16)]
    all_to_all x3 -> x0, starting transfers between devices: 16.1 us -> none  [the longest x2 10.2 us: exchange_columns(): lax.all_to_all(narrow, 'rows', split_axis=0, concat_axis=0, tiled=True)]
    transpose x2 -> x0, local copies, waits for them, and re-layouts: 15.8 us -> none  [exchange_columns(): return arrived.transpose(1, 0, 2, 3).reshape(experts, parts * depth, width)]
  transfers between devices with their start and end apart: 3 -> 0, of which waited for: 3 -> 0; matrix products, arithmetic and copies ran while one was open for 3% -> 0% of each run, Pallas kernels for 3% -> 0%
where the time goes in v1:
time: 572 us
  Pallas kernels  559 us (98%)
  local copies, waits for them, and re-layouts  12.1 us (2%)
    pallas_call x1, Pallas kernels, serve(): pl.pallas_call(serve_kernel, out_shape=(pltpu.VMEM((2 * experts, rows * d...  559 us

profile of v1, /device:TPU:0, one launch (start us, length us, event | category | flops | bytes accessed | tf_op | source)
XLA Modules:
  0.0 571.6 jit_solution(5411616570828018601)
XLA Ops:
  0.6 558.9 %shard_map.135 = (bf16[32,2048,128]{2,1,0:T(8,128)(2,1)S(1)}, bf16[16,128,2048]{2,1,0:T(8,128)(2,1)S(1)}, f32[16,128]{1,0:T(8,128)}, f32[16,128]{1,0:T(8,128)}, ...) custom-call(f32[16,256,1024]{2,1,0:T(8,128)} %master_gate.1, bf16[16,256,1024]{2,1,0:T(8,128)(2,1)} %second_gate.1, ...), custom_call_target="tpu_custom_call" | custom-call | flops 100663296 | bytes 150994944 | tf_op jit(solution)/shard_map/pallas_call | solution.py:439
  559.6 6.1 %fusion = (bf16[16,2048,128]{2,1,0:T(8,128)(2,1)}, bf16[16,2048,128]{2,1,0:T(8,128)(2,1)}) fusion(bf16[32,2048,128]{2,1,0:T(8,128)(2,1)S(1)} %get-tuple-element.13), kind=kLoop, calls=%fused_computation | loop fusion | bytes 33554432 | tf_op jit(solution)/shard_map/slice | solution.py:499
  565.7 0.0 copy-start.3
  565.7 0.0 copy-start.2
  565.7 0.0 copy-start.1
  565.7 0.0 copy-start
  565.7 3.4 copy.20
  569.1 0.0 copy-done.3
  569.1 0.6 copy.21
  569.7 0.0 copy-done.2
  569.7 0.6 copy.22
  570.3 0.0 copy-done.1
  570.3 0.6 copy.23
  570.9 0.0 copy-done
  570.9 0.7 copy.24
Async XLA Ops:
  565.7 3.4 copy-start.3
  565.7 4.0 copy-start.2
  565.7 4.6 copy-start.1
  565.7 5.2 copy-start

commit v2 on v1

--- a/solution.py
+++ b/solution.py
@@ -42,8 +42,8 @@
 MESH = pl.DeviceIdType.MESH
 LANES = 128
 SLOTS = 3
-FIRST = 6
-EARLY = 3
+FIRST = 2
+FILL = 2
 
 
 def serve_kernel(
@@ -57,10 +57,10 @@
     router_gain,
     final_wide,
     final_down,
-    scale_gate,
-    scale_up,
-    scale_down,
+    scale_all,
     serve_router,
+    held_master,
+    held_second,
     wide_master,
     wide_second,
     tall_master,
@@ -76,6 +76,7 @@
     scales,
     weight_vmem,
     gain_vmem,
+    held_sem,
     wide_sem,
     tall_sem,
     router_sem,
@@ -107,6 +108,7 @@
     width = final_wide.shape[2]
     tall = final_down.shape[1]
     across = master_down.shape[2]
+    sent_copies = []
 
     def row_peer(step):
         return lax.rem(me + step, rows)
@@ -133,49 +135,59 @@
             device_id_type=MESH,
         )
 
+    def post(source, target, sent, arrived, place):
+        copy = remote(source, target, sent, arrived, place)
+        copy.start()
+        sent_copies.append(copy)
+        return copy
+
     def fetch(pair, buffers, sems, expert, slot):
         return [
             pltpu.make_async_copy(pair[i].at[expert], buffers[i].at[slot], sems.at[i, slot])
             for i in range(2)
         ]
 
-    def ahead(pair, buffers, sems, first, count):
-        for i in range(min(SLOTS, count)):
-            for copy in fetch(pair, buffers, sems, first + i, i):
-                copy.start()
-
-    def run(pair, buffers, sems, first, count, work):
-        def step(i, _):
-            slot = lax.rem(i, SLOTS)
-            for copy in fetch(pair, buffers, sems, first + i, slot):
-                copy.wait()
-            work(first + i, slot)
-
-            @pl.when(i + SLOTS < count)
-            def _():
-                for copy in fetch(pair, buffers, sems, first + i + SLOTS, slot):
+    class Stream:
+        def __init__(self, pair, buffers, sems, first, last):
+            self.pair, self.buffers, self.sems = pair, buffers, sems
+            self.first, self.last = first, last
+            for i in range(min(SLOTS, last - first)):
+                for copy in fetch(pair, buffers, sems, first + i, i):
                     copy.start()
 
-            return 0
-
-        lax.fori_loop(0, count, step, 0)
-
+        def run(self, begin, end, work):
+            def step(expert, _):
+                slot = lax.rem(expert - self.first, SLOTS)
+                for copy in fetch(self.pair, self.buffers, self.sems, expert, slot):
+                    copy.wait()
+                work(expert, slot)
+
+                @pl.when(expert + SLOTS < self.last)
+                def _():
+                    for copy in fetch(self.pair, self.buffers, self.sems, expert + SLOTS, slot):
+                        copy.start()
+
+                return 0
+
+            lax.fori_loop(begin, end, step, 0)
+
+    held = (held_master, held_second)
     wide = (wide_master, wide_second)
     high = (tall_master, tall_second)
     gate = (master_gate, second_gate)
     up = (master_up, second_up)
     down = (master_down, second_down)
 
-    def wide_block(slot, part):
+    def wide_block(buffers, slot, part):
         columns = pl.ds(pl.multiple_of(part * width, width), width)
-        return wide_master[slot, :, columns] + wide_second[slot, :, columns].astype(jnp.float32)
+        return buffers[0][slot, :, columns] + buffers[1][slot, :, columns].astype(jnp.float32)
 
     def tall_block(slot, part):
         lines = pl.ds(pl.multiple_of(part * tall, tall), tall)
         return tall_master[slot, lines, :] + tall_second[slot, lines, :].astype(jnp.float32)
 
-    def wide_total(slot, part):
-        merged = wide_block(slot, part)
+    def wide_total(slot, part, buffers=wide):
+        merged = wide_block(buffers, slot, part)
         return jnp.sum(merged * merged, axis=0, keepdims=True)
 
     def tall_total(slot, part):
@@ -186,10 +198,6 @@
             narrow = narrow + square[:, at : at + LANES]
         return jnp.sum(narrow.T, axis=0, keepdims=True)
 
-    def sum_first(expert, slot):
-        for part in range(rows):
-            first_sums[me, expert, part : part + 1, :] = wide_total(slot, part)
-
     def sum_rest(total_of, offset):
         def work(expert, slot):
             for part in range(rows):
@@ -206,17 +214,23 @@
     my_lines = pl.ds(pl.multiple_of(me * depth, depth), depth)
     my_columns = pl.ds(pl.multiple_of(me * across, across), across)
 
-    def narrow_wide(scale_of, which):
+    def part_of(slot):
+        part, bit = 0, 1
+        while bit < rows:
+            part = part + bit * lax.rem(me // bit + 1 + slot // bit, 2)
+            bit = 2 * bit
+        return part
+
+    def narrow_wide(scale_of, which, buffers=wide, begin=0, end=rows - 1):
         def work(expert, slot):
             at = which * experts + expert
 
             def block(i, _):
-                step = rows - 1 - i
-                part = row_peer(step)
-                value = wide_block(slot, part) / scale_of(expert, part)
-                wide_send[at, step - 1] = value.astype(jnp.bfloat16)
+                part = part_of(i)
+                value = wide_block(buffers, slot, part) / scale_of(expert, part)
+                wide_send[at, i] = value.astype(jnp.bfloat16)
                 remote(
-                    wide_send.at[at, step - 1],
+                    wide_send.at[at, i],
                     final_wide.at[at, my_lines, :],
                     bulk_sent.at[which],
                     bulk_arrived.at[which],
@@ -224,9 +238,10 @@
                 ).start()
                 return 0
 
-            lax.fori_loop(0, rows - 1, block, 0)
-            own = wide_block(slot, me) / scale_of(expert, me)
-            final_wide[at, my_lines, :] = own.astype(jnp.bfloat16)
+            lax.fori_loop(begin, end, block, 0)
+            if end == rows - 1:
+                own = wide_block(buffers, slot, me) / scale_of(expert, me)
+                final_wide[at, my_lines, :] = own.astype(jnp.bfloat16)
 
         return work
 
@@ -240,11 +255,10 @@
         scale_of = rest_scale(2 * experts)
 
         def block(i, _):
-            step = rows - 1 - i
-            part = row_peer(step)
-            tall_send[expert, step - 1] = narrow_tall(slot, part, scale_of(expert, part))
+            part = part_of(i)
+            tall_send[expert, i] = narrow_tall(slot, part, scale_of(expert, part))
             remote(
-                tall_send.at[expert, step - 1],
+                tall_send.at[expert, i],
                 final_down.at[expert, :, my_columns],
                 bulk_sent.at[2],
                 bulk_arrived.at[2],
@@ -255,19 +269,74 @@
         lax.fori_loop(0, rows - 1, block, 0)
         final_down[expert, :, my_columns] = narrow_tall(slot, me, scale_of(expert, me))
 
-    ahead(gate, wide, wide_sem, 0, FIRST)
+    my_parts = pl.ds(rank * per_rank, per_rank)
+
+    def send_near(which, lines):
+        copies = []
+        for step in range(1, half):
+            parts = pl.ds(lax.rem(rank + step, half) * per_rank, per_rank)
+            copies.append(
+                post(
+                    sums.at[parts, lines],
+                    half_sums.at[rank, :, lines],
+                    near_sent.at[which, step - 1],
+                    near_arrived.at[which, step - 1],
+                    {"rows": half_peer(step)},
+                )
+            )
+        half_sums[rank, :, lines] = sums[my_parts, lines]
+        return copies
+
+    def send_across(which, lines, copies):
+        for copy in copies:
+            copy.wait_recv()
+        total = half_sums[0, :, lines]
+        for part in range(1, half):
+            total = total + half_sums[part, :, lines]
+        half_total[:, lines] = total
+        return post(
+            half_total.at[:, lines],
+            other_total.at[:, lines],
+            across_sent.at[which],
+            across_arrived.at[which],
+            {"rows": mirror},
+        )
+
+    def send_back(which, lines, copy):
+        copy.wait_recv()
+        scales[my_parts, lines] = jnp.sqrt(half_total[:, lines] + other_total[:, lines])
+        place = scales.at[my_parts, lines]
+        return [
+            post(
+                place,
+                place,
+                back_sent.at[which, step - 1],
+                back_arrived.at[which, step - 1],
+                {"rows": half_peer(step)},
+            )
+            for step in range(1, half)
+        ]
+
+    for expert in range(FIRST):
+        for copy in fetch(gate, held, held_sem, expert, expert):
+            copy.start()
+    stream = Stream(gate, wide, wide_sem, FIRST, experts)
     fetch_router = [
         pltpu.make_async_copy(router_weight, weight_vmem, router_sem.at[0]),
         pltpu.make_async_copy(router_gain, gain_vmem, router_sem.at[1]),
     ]
     for copy in fetch_router:
         copy.start()
-    sums[...] = jnp.zeros_like(sums)
-    run(gate, wide, wide_sem, 0, FIRST, sum_first)
-    ahead(gate, wide, wide_sem, 0, EARLY)
+    for part in range(rows):
+        sums[part, 0:8, :] = jnp.zeros((8, LANES), jnp.float32)
+    for expert in range(FIRST):
+        for copy in fetch(gate, held, held_sem, expert, expert):
+            copy.wait()
+        for part in range(rows):
+            first_sums[me, expert, part : part + 1, :] = wide_total(expert, part, held)
     pl.semaphore_wait(barrier, rows - 1 + owners - 1)
     first_copies = [
-        remote(
+        post(
             first_sums.at[me],
             first_sums.at[me],
             first_sent.at[step - 1],
@@ -276,8 +345,32 @@
         )
         for step in range(1, rows)
     ]
+    sum_gate = sum_rest(wide_total, 0)
+    stream.run(FIRST, FIRST + FILL, sum_gate)
     for copy in first_copies:
-        copy.start()
+        copy.wait_recv()
+    total = first_sums[0]
+    for part in range(1, rows):
+        total = total + first_sums[part]
+    first_scales[...] = jnp.sqrt(total)
+
+    middle = rows // 2
+    early = narrow_wide(first_scale, 0, held, 0, middle)
+    late = narrow_wide(first_scale, 0, held, middle, rows - 1)
+    lines = pl.ds(0, experts)
+    early(0, 0)
+    stream.run(FIRST + FILL, experts, sum_gate)
+    copies = send_near(0, lines)
+    late(0, 0)
+    near_end = experts // 2
+    stream = Stream(gate, wide, wide_sem, FIRST, near_end)
+    copy = send_across(0, lines, copies)
+    for expert in range(1, FIRST - 1):
+        early(expert, expert)
+        late(expert, expert)
+    early(FIRST - 1, FIRST - 1)
+    copies = send_back(0, lines, copy)
+    late(FIRST - 1, FIRST - 1)
 
     for copy in fetch_router:
         copy.wait()
@@ -288,87 +381,38 @@
     serve_router[my_experts, here] = (weight_vmem[...] * gain_vmem[...]).astype(jnp.bfloat16)
     my_route = serve_router.at[my_experts, here]
     other_route = serve_router.at[my_experts, there]
-    route_copies = [remote(my_route, my_route, route_sent.at[0], route_arrived.at[0], {"rows": mirror})]
-    route_copies[0].start()
-
-    for copy in first_copies:
+    mirrored = post(my_route, my_route, route_sent.at[0], route_arrived.at[0], {"rows": mirror})
+
+    for copy in copies:
         copy.wait_recv()
-    total = first_sums[0]
-    for part in range(1, rows):
-        total = total + first_sums[part]
-    first_scales[...] = jnp.sqrt(total)
-    narrow_first = narrow_wide(first_scale, 0)
-    run(gate, wide, wide_sem, 0, EARLY, narrow_first)
-
-    sum_gate = sum_rest(wide_total, 0)
-    sum_up = sum_rest(wide_total, experts)
-    sum_down = sum_rest(tall_total, 2 * experts)
-    ahead(gate, wide, wide_sem, FIRST, experts - FIRST)
-    ahead(down, high, tall_sem, 0, experts)
-    run(gate, wide, wide_sem, FIRST, experts - FIRST, sum_gate)
-    ahead(up, wide, wide_sem, 0, experts)
-    run(down, high, tall_sem, 0, experts, sum_down)
-    run(up, wide, wide_sem, 0, experts, sum_up)
-
-    ahead(gate, wide, wide_sem, EARLY, 1)
-    near_copies = []
-    for step in range(1, half):
-        peer = half_peer(step)
-        peer_rank = lax.rem(rank + step, half)
-        near_copies.append(
-            remote(
-                sums.at[pl.ds(peer_rank * per_rank, per_rank)],
-                half_sums.at[rank],
-                near_sent.at[step - 1],
-                near_arrived.at[step - 1],
-                {"rows": peer},
-            )
-        )
-        near_copies[-1].start()
-    half_sums[rank] = sums[pl.ds(rank * per_rank, per_rank)]
-    run(gate, wide, wide_sem, EARLY, 1, narrow_first)
-    ahead(gate, wide, wide_sem, EARLY + 1, 1)
-    for copy in near_copies:
-        copy.wait_recv()
-    total = half_sums[0]
-    for part in range(1, half):
-        total = total + half_sums[part]
-    half_total[...] = total
-    across_copy = remote(half_total, other_total, across_sent.at[0], across_arrived.at[0], {"rows": mirror})
-    across_copy.start()
-    route_copies[0].wait_recv()
+    narrow_gate = narrow_wide(rest_scale(0), 0)
+    stream.run(FIRST, near_end, narrow_gate)
+
+    stream = Stream(up, wide, wide_sem, 0, experts)
+    other = Stream(down, high, tall_sem, 0, experts)
+    stream.run(0, experts, sum_rest(wide_total, experts))
+    stream = Stream(gate, wide, wide_sem, near_end, experts)
+    other.run(0, experts, sum_rest(tall_total, 2 * experts))
+    other = Stream(down, high, tall_sem, 0, experts)
+    lines = pl.ds(experts, 2 * experts)
+    copies = send_near(1, lines)
+    stream.run(near_end, near_end + 2, narrow_gate)
+    copy = send_across(1, lines, copies)
+    mirrored.wait_recv()
+    routes = []
     for step in range(1, half):
         for i, route in enumerate((my_route, other_route)):
             at = 1 + 2 * (step - 1) + i
-            route_copies.append(
-                remote(route, route, route_sent.at[at], route_arrived.at[at], {"rows": half_peer(step)})
+            routes.append(
+                post(route, route, route_sent.at[at], route_arrived.at[at], {"rows": half_peer(step)})
             )
-            route_copies[-1].start()
-    run(gate, wide, wide_sem, EARLY + 1, 1, narrow_first)
-    ahead(gate, wide, wide_sem, EARLY + 2, FIRST - EARLY - 2)
-    across_copy.wait_recv()
-    my_parts = pl.ds(rank * per_rank, per_rank)
-    scales[my_parts] = jnp.sqrt(half_total[...] + other_total[...])
-    back_copies = [
-        remote(
-            scales.at[my_parts],
-            scales.at[my_parts],
-            back_sent.at[step - 1],
-            back_arrived.at[step - 1],
-            {"rows": half_peer(step)},
-        )
-        for step in range(1, half)
-    ]
-    for copy in back_copies:
-        copy.start()
-    run(gate, wide, wide_sem, EARLY + 2, FIRST - EARLY - 2, narrow_first)
-    ahead(gate, wide, wide_sem, FIRST, experts - FIRST)
-    ahead(down, high, tall_sem, 0, experts)
-    for copy in route_copies[1:]:
+    stream.run(near_end + 2, near_end + 4, narrow_gate)
+    copies = send_back(1, lines, copy)
+    for copy in routes:
         copy.wait_recv()
     owner_route = serve_router.at[my_experts, :]
     owner_copies = [
-        remote(
+        post(
             owner_route,
             owner_route,
             owner_sent.at[step - 1],
@@ -377,27 +421,23 @@
         )
         for step in range(1, owners)
     ]
-    for copy in owner_copies:
-        copy.start()
-    for copy in back_copies:
+    stream.run(near_end + 4, experts, narrow_gate)
+    stream = Stream(up, wide, wide_sem, 0, experts)
+    for copy in copies:
         copy.wait_recv()
 
-    run(gate, wide, wide_sem, FIRST, experts - FIRST, narrow_wide(rest_scale(0), 0))
-    ahead(up, wide, wide_sem, 0, experts)
-    run(up, wide, wide_sem, 0, experts, narrow_wide(rest_scale(experts), 1))
-    run(down, high, tall_sem, 0, experts, narrow_down)
-
-    scale_gate[...] = scales[me, 0:experts]
+    stream.run(0, experts, narrow_wide(rest_scale(experts), 1))
+    other.run(0, experts, narrow_down)
+
+    for which in range(3):
+        scale_all[which] = scales[me, which * experts : (which + 1) * experts]
     for expert in range(FIRST):
-        scale_gate[expert : expert + 1, :] = first_scale(expert, me)
-    scale_up[...] = scales[me, experts : 2 * experts]
-    scale_down[...] = scales[me, 2 * experts : 3 * experts]
+        scale_all[0, expert : expert + 1, :] = first_scale(expert, me)
 
     for copy in owner_copies:
         copy.wait_recv()
-    for copies in (first_copies, route_copies, near_copies, [across_copy], back_copies, owner_copies):
-        for copy in copies:
-            copy.wait_send()
+    for copy in sent_copies:
+        copy.wait_send()
     incoming = pl.ds(0, (rows - 1) * depth)
     arrived = (
         final_wide.at[pl.ds(0, experts), incoming, :],
@@ -410,6 +450,23 @@
         remote(sent[which], sent[which], bulk_sent.at[which], bulk_arrived.at[which], place).wait_send()
     for which in range(3):
         remote(arrived[which], arrived[which], bulk_sent.at[which], bulk_arrived.at[which], place).wait_recv()
+
+
+def deliver_kernel(wide, down, scale_all, router, gate_out, up_out, down_out, *rest):
+    scale_outs, router_out, sems = rest[:3], rest[3], rest[4]
+    experts = gate_out.shape[0]
+    pairs = [
+        (wide.at[pl.ds(0, experts)], gate_out),
+        (wide.at[pl.ds(experts, experts)], up_out),
+        (down, down_out),
+        (router, router_out),
+    ]
+    pairs += [(scale_all.at[i], scale_outs[i]) for i in range(3)]
+    copies = [pltpu.make_async_copy(*pair, sems.at[i]) for i, pair in enumerate(pairs)]
+    for copy in copies:
+        copy.start()
+    for copy in copies:
+        copy.wait()
 
 
 def serve(
@@ -436,19 +493,19 @@
     hbm = pl.BlockSpec(memory_space=pltpu.HBM)
     vmem = pl.BlockSpec(memory_space=pltpu.VMEM)
     size = 3 * experts * depth * columns
-    outs = pl.pallas_call(
+    arrived = pl.pallas_call(
         serve_kernel,
         out_shape=(
             pltpu.VMEM((2 * experts, rows * depth, width), bf16),
             pltpu.VMEM((experts, tall, rows * across), bf16),
-            jax.ShapeDtypeStruct((experts, width), f32),
-            jax.ShapeDtypeStruct((experts, width), f32),
-            jax.ShapeDtypeStruct((experts, tall), f32),
-            jax.ShapeDtypeStruct((owners * mine, rows * depth), bf16),
+            pltpu.VMEM((3, experts, width), f32),
+            pltpu.VMEM((owners * mine, rows * depth), bf16),
         ),
         in_specs=[hbm] * 8,
-        out_specs=(vmem,) * 6,
+        out_specs=(vmem,) * 4,
         scratch_shapes=[
+            pltpu.VMEM((FIRST, depth, columns), f32),
+            pltpu.VMEM((FIRST, depth, columns), bf16),
             pltpu.VMEM((SLOTS, depth, columns), f32),
             pltpu.VMEM((SLOTS, depth, columns), bf16),
             pltpu.VMEM((SLOTS, lines, across), f32),
@@ -464,6 +521,7 @@
             pltpu.VMEM((rows, chunks, LANES), f32),
             pltpu.VMEM((mine, depth), f32),
             pltpu.VMEM((1, depth), f32),
+            dma((2, FIRST)),
             dma((2, SLOTS)),
             dma((2, SLOTS)),
             dma((2,)),
@@ -471,19 +529,19 @@
             dma((3,)),
             dma((rows - 1,)),
             dma((rows - 1,)),
-            dma((half - 1,)),
-            dma((half - 1,)),
-            dma((1,)),
-            dma((1,)),
-            dma((half - 1,)),
-            dma((half - 1,)),
+            dma((2, half - 1)),
+            dma((2, half - 1)),
+            dma((2,)),
+            dma((2,)),
+            dma((2, half - 1)),
+            dma((2, half - 1)),
             dma((2 * half - 1,)),
             dma((2 * half - 1,)),
             dma((owners - 1,)),
             dma((owners - 1,)),
         ],
         compiler_params=pltpu.CompilerParams(
-            collective_id=0, has_side_effects=True, vmem_limit_bytes=34 * 1024 * 1024
+            collective_id=0, has_side_effects=True, vmem_limit_bytes=36 * 1024 * 1024
         ),
         cost_estimate=pl.CostEstimate(flops=8 * size, bytes_accessed=12 * size, transcendentals=0),
     )(
@@ -496,8 +554,24 @@
         router_weight.T,
         jnp.expand_dims(router_gain, 0),
     )
-    final_gate, final_up = outs[0][:experts], outs[0][experts:]
-    return (final_gate, final_up, *outs[1:5], outs[5].T)
+    outs = pl.pallas_call(
+        deliver_kernel,
+        out_shape=(
+            jax.ShapeDtypeStruct((experts, rows * depth, width), bf16),
+            jax.ShapeDtypeStruct((experts, rows * depth, width), bf16),
+            jax.ShapeDtypeStruct((experts, tall, rows * across), bf16),
+            jax.ShapeDtypeStruct((experts, width), f32),
+            jax.ShapeDtypeStruct((experts, width), f32),
+            jax.ShapeDtypeStruct((experts, tall), f32),
+            jax.ShapeDtypeStruct((owners * mine, rows * depth), bf16),
+        ),
+        in_specs=[vmem] * 4,
+        out_specs=(hbm,) * 7,
+        scratch_shapes=[dma((7,))],
+        compiler_params=pltpu.CompilerParams(vmem_limit_bytes=2 * 1024 * 1024),
+        cost_estimate=pl.CostEstimate(flops=size, bytes_accessed=4 * size, transcendentals=0),
+    )(*arrived)
+    return (*outs[:6], outs[6].T)
 
 
 def serve_fits(experts, depth, columns, lines, across, mine, rows):
@@ -509,7 +583,7 @@
         and depth % LANES == 0
         and experts % 16 == 0
         and mine % 16 == 0
-        and experts > FIRST
+        and experts >= FIRST + FILL
     )
 
 

time: 572 us -> 565 us (0.988)
  local copies, waits for them, and re-layouts: 12.1 us -> 0 us
    pallas_call x0 -> x1, Pallas kernels: none -> 8.75 us  [serve(): pl.pallas_call(deliver_kernel, out_shape=(jax.ShapeDtypeStruct((experts,...]
    slice x1 -> x0, local copies, waits for them, and re-layouts: 6.15 us -> none  [serve(): final_gate, final_up = (outs[0][:experts], outs[0][experts:])]
    unnamed x13 -> x0, local copies, waits for them, and re-layouts: 5.91 us -> none
where the time goes in v2:
time: 565 us; the launch traced here: 564 us
  Pallas kernels  564 us (100%)
    pallas_call x1, Pallas kernels, serve(): pl.pallas_call(serve_kernel, out_shape=(pltpu.VMEM((2 * experts, rows * d...  555 us

profile of v2, /device:TPU:0, one launch (start us, length us, event | category | flops | bytes accessed | tf_op | source)
XLA Modules:
  0.0 564.3 jit_solution(3478602355752764841)
XLA Ops:
  0.6 554.9 %shard_map.135 = (bf16[32,2048,128]{2,1,0:T(8,128)(2,1)S(1)}, bf16[16,128,2048]{2,1,0:T(8,128)(2,1)S(1)}, f32[3,16,128]{2,1,0:T(8,128)S(1)}, bf16[64,2048]{1,0:T(8,128)(2,1)S(1)}) custom-call(f32[16,256,1024]{2,1,0:T(8,128)} %master_gate.1, bf16[16,256,1024]{2,1,0:T(8,128)(2,1)} %second_gate.1, f32[16,256,1024]{2,1,0:T(8,128)} %master_up.1, ...), custom_call_target="tpu_custom_call" | custom-call | flops 100663296 | bytes 150994944 | tf_op jit(solution)/shard_map/pallas_call | solution.py:496
  555.5 8.8 %shard_map.136 = (bf16[16,2048,128]{2,1,0:T(8,128)(2,1)}, bf16[16,2048,128]{2,1,0:T(8,128)(2,1)}, bf16[16,128,2048]{2,1,0:T(8,128)(2,1)}, f32[16,128]{1,0:T(8,12...) custom-call(bf16[32,2048,128]{2,1,0:T(8,128)(2,1)S(1)} %get-tuple-element.18.wide, ...), custom_call_target="tpu_custom_call" | custom-call | flops 12582912 | bytes 50331648 | tf_op jit(solution)/shard_map/pallas_call | solution.py:557

commit v3 on v2

--- a/solution.py
+++ b/solution.py
@@ -1,3 +1,5 @@
+import functools
+
 import jax
 import jax.numpy as jnp
 from jax import lax
@@ -43,7 +45,8 @@
 LANES = 128
 SLOTS = 3
 FIRST = 2
-FILL = 2
+SECOND = 8
+PIECES = 4
 
 
 def serve_kernel(
@@ -221,6 +224,10 @@
             bit = 2 * bit
         return part
 
+    def last_part_of(slot):
+        across_part = lax.rem(base + half, rows) + slot
+        return jnp.where(slot < half, across_part, base + lax.rem(rank + slot + 1, half))
+
     def narrow_wide(scale_of, which, buffers=wide, begin=0, end=rows - 1):
         def work(expert, slot):
             at = which * experts + expert
@@ -251,11 +258,11 @@
         scale = jnp.concatenate([scale] * (across // LANES), axis=1)
         return (merged / scale).astype(jnp.bfloat16)
 
-    def narrow_down(expert, slot):
+    def narrow_down(expert, slot, part_at=part_of):
         scale_of = rest_scale(2 * experts)
 
         def block(i, _):
-            part = part_of(i)
+            part = part_at(i)
             tall_send[expert, i] = narrow_tall(slot, part, scale_of(expert, part))
             remote(
                 tall_send.at[expert, i],
@@ -320,7 +327,6 @@
     for expert in range(FIRST):
         for copy in fetch(gate, held, held_sem, expert, expert):
             copy.start()
-    stream = Stream(gate, wide, wide_sem, FIRST, experts)
     fetch_router = [
         pltpu.make_async_copy(router_weight, weight_vmem, router_sem.at[0]),
         pltpu.make_async_copy(router_gain, gain_vmem, router_sem.at[1]),
@@ -329,48 +335,26 @@
         copy.start()
     for part in range(rows):
         sums[part, 0:8, :] = jnp.zeros((8, LANES), jnp.float32)
+    first_copies = []
     for expert in range(FIRST):
         for copy in fetch(gate, held, held_sem, expert, expert):
             copy.wait()
         for part in range(rows):
             first_sums[me, expert, part : part + 1, :] = wide_total(expert, part, held)
-    pl.semaphore_wait(barrier, rows - 1 + owners - 1)
-    first_copies = [
-        post(
-            first_sums.at[me],
-            first_sums.at[me],
-            first_sent.at[step - 1],
-            first_arrived.at[step - 1],
-            {"rows": row_peer(step)},
+        if expert == 0:
+            pl.semaphore_wait(barrier, rows - 1 + owners - 1)
+        first_copies.append(
+            [
+                post(
+                    first_sums.at[me, expert],
+                    first_sums.at[me, expert],
+                    first_sent.at[expert, step - 1],
+                    first_arrived.at[expert, step - 1],
+                    {"rows": row_peer(step)},
+                )
+                for step in range(1, rows)
+            ]
         )
-        for step in range(1, rows)
-    ]
-    sum_gate = sum_rest(wide_total, 0)
-    stream.run(FIRST, FIRST + FILL, sum_gate)
-    for copy in first_copies:
-        copy.wait_recv()
-    total = first_sums[0]
-    for part in range(1, rows):
-        total = total + first_sums[part]
-    first_scales[...] = jnp.sqrt(total)
-
-    middle = rows // 2
-    early = narrow_wide(first_scale, 0, held, 0, middle)
-    late = narrow_wide(first_scale, 0, held, middle, rows - 1)
-    lines = pl.ds(0, experts)
-    early(0, 0)
-    stream.run(FIRST + FILL, experts, sum_gate)
-    copies = send_near(0, lines)
-    late(0, 0)
-    near_end = experts // 2
-    stream = Stream(gate, wide, wide_sem, FIRST, near_end)
-    copy = send_across(0, lines, copies)
-    for expert in range(1, FIRST - 1):
-        early(expert, expert)
-        late(expert, expert)
-    early(FIRST - 1, FIRST - 1)
-    copies = send_back(0, lines, copy)
-    late(FIRST - 1, FIRST - 1)
 
     for copy in fetch_router:
         copy.wait()
@@ -383,20 +367,49 @@
     other_route = serve_router.at[my_experts, there]
     mirrored = post(my_route, my_route, route_sent.at[0], route_arrived.at[0], {"rows": mirror})
 
+    stream = Stream(gate, wide, wide_sem, FIRST, SECOND)
+    sum_gate = sum_rest(wide_total, 0)
+    def total_first(expert):
+        for copy in first_copies[expert]:
+            copy.wait_recv()
+        total = first_sums[0, expert]
+        for part in range(1, rows):
+            total = total + first_sums[part, expert]
+        first_scales[expert] = jnp.sqrt(total)
+
+    def piece(expert, begin, end):
+        narrow_wide(first_scale, 0, held, begin, end)(expert, expert)
+
+    total_first(0)
+    piece(0, 0, half // 2)
+    stream.run(FIRST, SECOND, sum_gate)
+    lines = pl.ds(0, SECOND)
+    copies = send_near(0, lines)
+    stream = Stream(gate, wide, wide_sem, FIRST, SECOND - 3)
+    piece(0, half // 2, half)
+    copy = send_across(0, lines, copies)
+    total_first(1)
+    piece(1, 0, half // 2)
+    copies = send_back(0, lines, copy)
+    piece(0, half, rows - 1)
+    piece(1, half // 2, rows - 1)
+
     for copy in copies:
         copy.wait_recv()
     narrow_gate = narrow_wide(rest_scale(0), 0)
-    stream.run(FIRST, near_end, narrow_gate)
-
+    stream.run(FIRST, SECOND - 3, narrow_gate)
+
+    stream = Stream(gate, wide, wide_sem, SECOND, experts)
+    other = Stream(down, high, tall_sem, 0, experts)
+    stream.run(SECOND, experts, sum_gate)
     stream = Stream(up, wide, wide_sem, 0, experts)
+    other.run(0, experts, sum_rest(tall_total, 2 * experts))
     other = Stream(down, high, tall_sem, 0, experts)
     stream.run(0, experts, sum_rest(wide_total, experts))
-    stream = Stream(gate, wide, wide_sem, near_end, experts)
-    other.run(0, experts, sum_rest(tall_total, 2 * experts))
-    other = Stream(down, high, tall_sem, 0, experts)
-    lines = pl.ds(experts, 2 * experts)
+    stream = Stream(gate, wide, wide_sem, SECOND - 3, experts)
+    lines = pl.ds(SECOND, 3 * experts - SECOND)
     copies = send_near(1, lines)
-    stream.run(near_end, near_end + 2, narrow_gate)
+    stream.run(SECOND - 3, SECOND - 2, narrow_gate)
     copy = send_across(1, lines, copies)
     mirrored.wait_recv()
     routes = []
@@ -406,7 +419,7 @@
             routes.append(
                 post(route, route, route_sent.at[at], route_arrived.at[at], {"rows": half_peer(step)})
             )
-    stream.run(near_end + 2, near_end + 4, narrow_gate)
+    stream.run(SECOND - 2, SECOND - 1, narrow_gate)
     copies = send_back(1, lines, copy)
     for copy in routes:
         copy.wait_recv()
@@ -421,13 +434,15 @@
         )
         for step in range(1, owners)
     ]
-    stream.run(near_end + 4, experts, narrow_gate)
-    stream = Stream(up, wide, wide_sem, 0, experts)
+    stream.run(SECOND - 1, SECOND, narrow_gate)
     for copy in copies:
         copy.wait_recv()
+    stream.run(SECOND, experts, narrow_gate)
+    stream = Stream(up, wide, wide_sem, 0, experts)
 
     stream.run(0, experts, narrow_wide(rest_scale(experts), 1))
-    other.run(0, experts, narrow_down)
+    other.run(0, experts - 1, narrow_down)
+    other.run(experts - 1, experts, functools.partial(narrow_down, part_at=last_part_of))
 
     for which in range(3):
         scale_all[which] = scales[me, which * experts : (which + 1) * experts]
@@ -455,13 +470,12 @@
 def deliver_kernel(wide, down, scale_all, router, gate_out, up_out, down_out, *rest):
     scale_outs, router_out, sems = rest[:3], rest[3], rest[4]
     experts = gate_out.shape[0]
-    pairs = [
-        (wide.at[pl.ds(0, experts)], gate_out),
-        (wide.at[pl.ds(experts, experts)], up_out),
-        (down, down_out),
-        (router, router_out),
-    ]
-    pairs += [(scale_all.at[i], scale_outs[i]) for i in range(3)]
+    pairs = [(router, router_out)] + [(scale_all.at[i], scale_outs[i]) for i in range(3)]
+    size = experts // PIECES
+    for i in range(0, experts, size):
+        pairs.append((wide.at[pl.ds(i, size)], gate_out.at[pl.ds(i, size)]))
+        pairs.append((wide.at[pl.ds(experts + i, size)], up_out.at[pl.ds(i, size)]))
+        pairs.append((down.at[pl.ds(i, size)], down_out.at[pl.ds(i, size)]))
     copies = [pltpu.make_async_copy(*pair, sems.at[i]) for i, pair in enumerate(pairs)]
     for copy in copies:
         copy.start()
@@ -527,8 +541,8 @@
             dma((2,)),
             dma((3,)),
             dma((3,)),
-            dma((rows - 1,)),
-            dma((rows - 1,)),
+            dma((FIRST, rows - 1)),
+            dma((FIRST, rows - 1)),
             dma((2, half - 1)),
             dma((2, half - 1)),
             dma((2,)),
@@ -567,7 +581,7 @@
         ),
         in_specs=[vmem] * 4,
         out_specs=(hbm,) * 7,
-        scratch_shapes=[dma((7,))],
+        scratch_shapes=[dma((4 + 3 * PIECES,))],
         compiler_params=pltpu.CompilerParams(vmem_limit_bytes=2 * 1024 * 1024),
         cost_estimate=pl.CostEstimate(flops=size, bytes_accessed=4 * size, transcendentals=0),
     )(*arrived)
@@ -583,7 +597,7 @@
         and depth % LANES == 0
         and experts % 16 == 0
         and mine % 16 == 0
-        and experts >= FIRST + FILL
+        and experts >= SECOND
     )
 
 

time: 565 us -> 560 us (level)
  no operation moved by 1% of the time
where the time goes in v3:
time: 560 us
  Pallas kernels  559 us (100%)
    pallas_call x1, Pallas kernels, serve(): pl.pallas_call(serve_kernel, out_shape=(pltpu.VMEM((2 * experts, rows * d...  550 us

profile of v3, /device:TPU:0, one launch (start us, length us, event | category | flops | bytes accessed | tf_op | source)
XLA Modules:
  0.0 559.7 jit_solution(13818086197914764470)
XLA Ops:
  0.6 550.4 %shard_map.135 = (bf16[32,2048,128]{2,1,0:T(8,128)(2,1)S(1)}, bf16[16,128,2048]{2,1,0:T(8,128)(2,1)S(1)}, f32[3,16,128]{2,1,0:T(8,128)S(1)}, bf16[64,2048]{1,0:T(8,128)(2,1)S(1)}) custom-call(f32[16,256,1024]{2,1,0:T(8,128)} %master_gate.1, bf16[16,256,1024]{2,1,0:T(8,128)(2,1)} %second_gate.1, f32[16,256,1024]{2,1,0:T(8,128)} %master_up.1, ...), custom_call_target="tpu_custom_call" | custom-call | flops 100663296 | bytes 150994944 | tf_op jit(solution)/shard_map/pallas_call | solution.py:510
  551.1 8.6 %shard_map.136 = (bf16[16,2048,128]{2,1,0:T(8,128)(2,1)}, bf16[16,2048,128]{2,1,0:T(8,128)(2,1)}, bf16[16,128,2048]{2,1,0:T(8,128)(2,1)}, f32[16,128]{1,0:T(8,12...) custom-call(bf16[32,2048,128]{2,1,0:T(8,128)(2,1)S(1)} %get-tuple-element.18.wide, ...), custom_call_target="tpu_custom_call" | custom-call | flops 12582912 | bytes 50331648 | tf_op jit(solution)/shard_map/pallas_call | solution.py:571
